TPU v7x, 32 devices: a whole 2x2x4 slice. The times are simulated.
32 devices in a mesh: data: 2 (over x), hid: 4 (over z), vocab: 4 (over y, core).
Axes of the slice: x: 2, y: 2, z: 4, core: 2. Of those that a mesh axis runs over, the one named last changes fastest.
Arguments:
- h_states: bfloat16 [64, 1152], P('data', 'hid'), parts along dimension 0
- w_head: bfloat16 [1152, 262144], P('hid', 'vocab')
- inv_temp: float32 [64], P('data'), parts along dimension 0
- tgt_ids: int32 [64], P('data'), parts along dimension 0
Outputs:
- output 1: float32 [64, 262144], P('data', ('vocab', 'hid')), parts along dimension 0
- output 2: float32 [64], P('data'), parts along dimension 0
There are 2 independent parts. A program takes and returns all parts, laid end to end along the dimension named above; an argument that names none is the same for every part.
All inputs are finite; a program needn't handle non-finite values.
Results may differ from a plain program's by a relative error of at most 0.001.
Values are sent between devices in bfloat16 or wider.
A program may use at most 1 GiB of HBM per device.

v0:
```python
import jax
import jax.numpy as jnp
from jax import lax
from jax.sharding import PartitionSpec as P


def solution(mesh):
    hid_size = mesh.shape["hid"]
    voc_size = mesh.shape["vocab"]

    def local_step(h_blk, w_blk, temp_blk, tgt_blk):
        part_logits = jnp.dot(h_blk, w_blk, preferred_element_type=jnp.float32)
        logits = lax.psum_scatter(part_logits, "hid", scatter_dimension=1, tiled=True) * temp_blk[:, None]
        local_cols = logits.shape[1]
        glob_max = lax.pmax(jnp.max(logits, axis=1), ("vocab", "hid"))
        exp_vals = jnp.exp(logits - glob_max[:, None])
        glob_sum = lax.psum(jnp.sum(exp_vals, axis=1), ("vocab", "hid"))
        local_cdf = jnp.cumsum(exp_vals / glob_sum[:, None], axis=1)
        hid_tots = lax.all_gather(local_cdf[:, -1], "hid")
        vocab_tots = lax.all_gather(jnp.sum(hid_tots, axis=0), "vocab")
        hid_idx = lax.axis_index("hid")
        voc_idx = lax.axis_index("vocab")
        hid_off = jnp.sum(jnp.where((jnp.arange(hid_size) < hid_idx)[:, None], hid_tots, 0.0), axis=0)
        voc_off = jnp.sum(jnp.where((jnp.arange(voc_size) < voc_idx)[:, None], vocab_tots, 0.0), axis=0)
        cdf_blk = local_cdf + (voc_off + hid_off)[:, None]
        col_start = (voc_idx * hid_size + hid_idx) * local_cols
        local_pos = tgt_blk - col_start
        in_range = (local_pos >= 0) & (local_pos < local_cols)
        picked = jnp.take_along_axis(cdf_blk, jnp.clip(local_pos, 0, local_cols - 1)[:, None], axis=1)[:, 0]
        cdf_tgt = lax.psum(jnp.where(in_range, picked, 0.0), ("vocab", "hid"))
        return cdf_blk, cdf_tgt

    return jax.shard_map(local_step, mesh=mesh, in_specs=(P("data", "hid"), P("hid", "vocab"), P("data"), P("data")), out_specs=(P("data", ("vocab", "hid")), P("data")), check_vma=False)
```

profile of v0, /device:TPU:16, one launch (start us, length us, event | category | flops | bytes accessed | tf_op | source)
XLA Modules:
  0.0 302.0 jit_solution(2488027927748528559)
XLA Ops:
  7.2 0.0 reduce-scatter.2.cloned.1.call-start
  7.2 0.7 copy-done
  7.9 18.8 %fusion.3 = f32[32,65536]{1,0:T(8,128)} fusion(bf16[32,288]{1,0:T(8,128)(2,1)S(1)} %copy-done, bf16[288,65536]{1,0:T(8,128)(2,1)} %param.5), kind=kOutput, calls=%fused_computation.21 | convolution fusion | flops 1207959552 | bytes 46155776 | tf_op jit(solution)/shard_map/dot_general | solution.py:12
  26.7 0.0 reduce-scatter.2.cloned.1.call-update
  26.7 0.6 copy-done.5
  27.3 0.6 dynamic-slice
  27.9 0.6 dynamic-slice.1
  29.9 142.3 %reduce-scatter.2.cloned.1.call-done = f32[32,16384]{1,0:T(8,128)} async-done(((f32[32,65536]{1,0:T(8,128)}), f32[32,16384]{1,0:T(8,128)}) %reduce-scatter.2.cloned.1.call-update) | async-done | bytes 2097168 | tf_op jit(solution)/shard_map/reduce_scatter | solution.py:13
  172.2 2.1 multiply_reduce_fusion
  174.3 29.2 %pmax.7 = f32[32]{0:T(128)S(1)} all-reduce(f32[32]{0:T(128)S(1)} %multiply_reduce_fusion), channel_id=1, replica_groups=mesh['data'=2,'hid'=4,'vocab'=4] {'vocab','hid'}, use_global_device_ids=true, to_apply=%region_2.0 | all-reduce | flops 32 | bytes 256 | tf_op jit(solution)/shard_map/pmax | solution.py:15
  203.4 0.6 fusion
  204.0 29.7 %psum.14 = f32[32]{0:T(128)S(1)} all-reduce(f32[32]{0:T(128)S(1)} %fusion), channel_id=1, replica_groups=mesh['data'=2,'hid'=4,'vocab'=4] {'vocab','hid'}, use_global_device_ids=true, to_apply=%region_4.0 | all-reduce | flops 32 | bytes 256 | tf_op jit(solution)/shard_map/psum | solution.py:17
  233.7 0.4 divide_bitcast_fusion
  234.1 0.4 copy.9
  234.5 2.0 copy.7
  236.4 1.8 fusion.2
  238.2 0.3 reduce-window.9
  238.5 1.6 broadcast_add_fusion.1
  240.1 2.0 copy.8
  242.1 1.2 copy.14
  243.3 0.2 slice_reduce_fusion
  243.5 0.2 dynamic-update-slice
  243.7 10.6 %all-reduce = f32[128]{0:T(128)S(1)} all-reduce(f32[128]{0:T(128)S(1)} %dynamic-update-slice), channel_id=2, replica_groups=mesh['data'=2,'hid'=4,'vocab'=4] {'hid'}, use_global_device_ids=true, to_apply=%add | all-reduce | flops 128 | bytes 1024
  254.4 0.1 reshape.63
  254.5 0.1 select_reduce_fusion
  254.6 0.2 dynamic-update-slice.1
  254.8 5.6 %all-reduce.1 = f32[128]{0:T(128)S(1)} all-reduce(f32[128]{0:T(128)S(1)} %dynamic-update-slice.1), channel_id=3, replica_groups=mesh['data'=2,'hid'=4,'vocab'=4] {'vocab'}, use_global_device_ids=true, to_apply=%add.1 | all-reduce | flops 128 | bytes 1024
  260.4 0.1 reshape.64
  260.5 0.1 select_reduce_fusion.1
  260.6 2.5 broadcast_add_fusion
  263.1 1.9 gather_fusion
  265.1 30.1 %psum.15 = f32[32]{0:T(128)} all-reduce(f32[32]{0:T(128)S(1)} %and_select_fusion.1), channel_id=1, replica_groups=mesh['data'=2,'hid'=4,'vocab'=4] {'vocab','hid'}, use_global_device_ids=true, to_apply=%region_10.11 | all-reduce | flops 32 | bytes 256 | tf_op jit(solution)/shard_map/psum | solution.py:30
  (22 shorter events, 0.1 us)
Async XLA Ops:
  7.2 0.7 copy-start
  7.2 165.0 %reduce-scatter.2.cloned.1.call-start = ((), (), s32[]{:S(2)}) async-start(), calls=%async_computation.1 | async-start | bytes 10485760 | tf_op jit(solution)/shard_map/reduce_scatter | solution.py:13
  26.7 0.7 copy-start.5
  26.7 1.2 copy-start.4
  26.7 3.2 %copy-start.3 = (s32[32]{0:T(128)S(1)}, s32[32]{0:T(128)}, u32[]{:S(2)}) copy-start(s32[32]{0:T(128)} %param.7) | copy-start | bytes 388
  26.7 145.5 %copy-start.2 = (f32[32]{0:T(128)S(1)}, f32[32]{0:T(128)}, u32[]{:S(2)}) copy-start(f32[32]{0:T(128)} %param.6) | copy-start | bytes 388
  172.2 31.2 %copy-start.1 = (f32[32,16384]{1,0:T(8,128)S(1)}, f32[32,16384]{1,0:T(8,128)}, u32[]{:S(2)}) copy-start(f32[32,16384]{1,0:T(8,128)} %reduce-scatter.2.cloned.1.call-done) | copy-start | bytes 6291460
Sparse Core Ops, SparseCore 0:
  26.8 145.3 reduce-scatter.1
where the time goes:
time: 307 us; the launch traced here: 302 us
  waiting for transfers between devices  142 us (46%)
  blocking collectives  105 us (34%)
  matrix products  18.8 us (6%)
  between operations  15.5 us (5%)
  local copies, waits for them, and re-layouts  10.8 us (4%)
  other arithmetic  9.4 us (3%)
    reduce_scatter x1, waiting for transfers between devices, local_step(): lax.psum_scatter(part_logits, 'hid', scatter_dimension=1, tiled=True)  142 us
    psum x1, blocking collectives, local_step(): cdf_tgt = lax.psum(jnp.where(in_range, picked, 0.0), ('vocab', 'hid'))  30.1 us
    psum x1, blocking collectives, local_step(): glob_sum = lax.psum(jnp.sum(exp_vals, axis=1), ('vocab', 'hid'))  29.7 us
    pmax x1, blocking collectives, local_step(): glob_max = lax.pmax(jnp.max(logits, axis=1), ('vocab', 'hid'))  29.2 us
    dot_general x1, matrix products, local_step(): part_logits = jnp.dot(h_blk, w_blk, preferred_element_type=jnp.float32)  18.8 us
    unnamed x2, blocking collectives  16.3 us
  transfers between devices with their start and end apart: 1, of which 1 were waited for; matrix products, arithmetic and copies ran while one was open for 0% of the time, Pallas kernels for 0%

commit v1 on v0

v1 whole, which is shorter than its diff:
```python
import functools

import jax
import jax.numpy as jnp
from jax import lax
from jax.experimental import pallas as pl
from jax.experimental.pallas import tpu as pltpu
from jax.sharding import PartitionSpec as P

MESH = pl.DeviceIdType.MESH
NP = 16
NX = 2
RING = 4
LAG = 2
XSTEP = 2 * NP + 4
F32 = jnp.float32
BF16 = jnp.bfloat16


def iota(shape, dim):
    return lax.broadcasted_iota(jnp.int32, shape, dim)


def to_col(row):
    n = row.shape[1]
    return jnp.sum(jnp.where(iota((32, n), 0) == iota((32, n), 1), row, 0.0), axis=1, keepdims=True)


def pack_row(m, s, t):
    sub, lane = iota((32, 128), 0), iota((32, 128), 1)
    picked = jnp.where(lane == sub, m, jnp.where(lane == sub + 32, s, jnp.where(lane == sub + 64, t, 0.0)))
    return jnp.sum(picked, axis=0, keepdims=True)


def kernel(tok, h_hbm, w_hbm, temp_ref, tgt_ref, out_ref, tgt_out_ref,
           h_buf, w_buf, part, far_in, side_in, near_in, x_part, x_src, x_in, piece_m, piece_s, piece_t,
           msg_src, msg_in, stats,
           h_sem, w_sem, far_send, far_recv, side_recv, near_send, near_recv, xp_send, xp_recv, x_send, x_recv,
           msg_send, msg_recv, st_send, st_recv):
    z, v = lax.axis_index("hid"), lax.axis_index("vocab")
    outer = (z == 0) | (z == 3)
    inner = (z == 1) | (z == 2)
    far = jnp.where(z < 2, z + 1, z - 1)
    near = jnp.where(z == 1, 0, 3)
    cols = NP * tok
    last = 3 * NP - NX

    def w_load(rel, i, slot):
        owner = jnp.where(z < 2, rel, 3 - rel)
        start = pl.multiple_of(owner * cols + i * tok, tok)
        return pltpu.make_async_copy(w_hbm.at[:, pl.ds(start, tok)], w_buf.at[slot], w_sem.at[slot])

    h_copy = pltpu.make_async_copy(h_hbm, h_buf, h_sem)
    h_copy.start()
    for slot, rel in enumerate((3, 0, 2, 1)):
        w_load(rel, 0, slot).start()

    barrier = pltpu.get_barrier_semaphore()
    for dv in range(4):
        for dz in range(4):
            if dv or dz:
                pl.semaphore_signal(barrier, inc=1, device_id={"hid": lax.rem(z + dz, 4), "vocab": lax.rem(v + dv, 4)},
                                    device_id_type=MESH)

    def product(rel, i, slot):
        w_load(rel, i, slot).wait()
        part[rel * NP + i] = jnp.dot(h_buf[...], w_buf[slot], preferred_element_type=F32)

        @pl.when(i + 1 < NP)
        def _():
            w_load(rel, i + 1, slot).start()

    def products(i):
        product(0, i, 1)
        product(2, i, 2)
        product(1, i, 3)

        @pl.when(i + 1 < NP)
        def _():
            product(3, i + 1, 0)

    tri = (iota((128, 128), 0) <= iota((128, 128), 1)).astype(BF16)
    piece_m[...] = jnp.zeros_like(piece_m)
    piece_s[...] = jnp.zeros_like(piece_s)
    piece_t[...] = jnp.zeros_like(piece_t)
    temp = to_col(temp_ref[...])
    tgt_row = tgt_ref[...].astype(F32)
    tgt = to_col(tgt_row)

    def put(ref, lane, value):
        ref[...] = jnp.where(iota((32, 128), 1) == lane, value, ref[...])

    def finish(total, first, lane, store):
        logits = total * temp
        m = jnp.max(logits, axis=1, keepdims=True)
        e = jnp.exp(logits - m)
        n_blk = tok // 128
        terms = []
        for b in range(n_blk):
            blk = e[:, b * 128:(b + 1) * 128]
            hi = blk.astype(BF16)
            rest = blk - hi.astype(F32)
            mid = rest.astype(BF16)
            low = (rest - mid.astype(F32)).astype(BF16)
            terms += [hi, mid, low]
        sums = jnp.dot(jnp.concatenate(terms, axis=0), tri, preferred_element_type=F32)
        carry = jnp.zeros((32, 1), F32)
        hit = jnp.zeros((32, 128), F32)
        pos = tgt - first
        lanes = iota((32, 128), 1).astype(F32)
        for b in range(n_blk):
            s = sums[96 * b:96 * b + 96]
            c = (s[0:32] + s[32:64] + s[64:96]) + carry
            store(b, c)
            hit = hit + jnp.where(lanes == pos - float(b * 128), c, 0.0)
            carry = c[:, 127:128]
        put(piece_m, lane, m)
        put(piece_s, lane, carry)
        put(piece_t, lane, jnp.sum(hit, axis=1, keepdims=True))

    def first_token(owner, i):
        return (((v * 4 + owner) * NP + i) * tok).astype(F32)

    def scan_lanes(x):
        lane = iota((32, 128), 1)
        for shift in (1, 2, 4, 8):
            x = x + jnp.where(lane >= shift, pltpu.roll(x, shift, 1), 0.0)
        return x

    def combine(owner):
        lane = iota((32, 128), 1)
        live = lane < NP
        m_all, s_all, t_all = piece_m[...], piece_s[...], piece_t[...]
        m = jnp.max(jnp.where(live, m_all, m_all[:, 0:1]), axis=1, keepdims=True)
        scale = jnp.where(live, jnp.exp(jnp.where(live, m_all, m) - m), 0.0)
        tot = s_all * scale
        s = jnp.sum(tot, axis=1, keepdims=True)
        low = lane.astype(F32) * float(tok) + first_token(owner, 0)
        t = jnp.sum(jnp.where(low + float(tok) <= tgt, tot, jnp.where(low <= tgt, t_all * scale, 0.0)),
                    axis=1, keepdims=True)
        return pack_row(m, s, t)

    def far_copy(src, t, dst, sems):
        return pltpu.make_async_remote_copy(src_ref=src, dst_ref=dst.at[t], send_sem=far_send.at[lax.rem(t, RING)],
                                            recv_sem=sems.at[t], device_id={"hid": far}, device_id_type=MESH)

    def outer_copy(t):
        i, ph = lax.rem(t, NP), t // NP
        return far_copy(part.at[(3 - ph) * NP + i], t, far_in, far_recv)

    def inner_copy(t):
        return far_copy(far_in.at[t], t, side_in, side_recv)

    def near_copy(g):
        return pltpu.make_async_remote_copy(src_ref=side_in.at[g], dst_ref=near_in.at[g],
                                            send_sem=near_send.at[lax.rem(g, RING)], recv_sem=near_recv.at[g],
                                            device_id={"hid": near}, device_id_type=MESH)

    def x_part_copy(k):
        return pltpu.make_async_remote_copy(src_ref=side_in.at[2 * NP - NX + k], dst_ref=x_part.at[k],
                                            send_sem=xp_send.at[k], recv_sem=xp_recv.at[k],
                                            device_id={"hid": near}, device_id_type=MESH)

    def x_copy(k):
        return pltpu.make_async_remote_copy(src_ref=x_src.at[k], dst_ref=x_in.at[k], send_sem=x_send.at[k],
                                            recv_sem=x_recv.at[k], device_id={"hid": far}, device_id_type=MESH)

    msg_copy = pltpu.make_async_remote_copy(src_ref=msg_src, dst_ref=msg_in, send_sem=msg_send, recv_sem=msg_recv,
                                            device_id={"hid": far}, device_id_type=MESH)

    h_copy.wait()
    product(3, 0, 0)
    pl.semaphore_wait(barrier, 15)

    def out_store(i):
        def store(b, c):
            out_ref[:, pl.ds(pl.multiple_of(i * tok + b * 128, 128), 128)] = c
        return store

    @pl.when(outer)
    def _():
        def step(t, _):
            i = lax.rem(t, NP)

            @pl.when(t >= RING)
            def _():
                outer_copy(t - RING).wait_send()

            outer_copy(t).start()

            @pl.when(t < NP)
            def _():
                products(i)

            @pl.when((t >= NP) & (t < 2 * NP))
            def _():
                near_copy(i).wait_recv()
                finish(part[i] + near_in[i], first_token(z, i), i, out_store(i))

            @pl.when(t == XSTEP)
            def _():
                for k in range(NX):
                    def store(b, c, k=k):
                        x_src[k, :, b * 128:(b + 1) * 128] = c
                    x_part_copy(k).wait_recv()
                    finish(part[2 * NP - NX + k] + x_part[k], first_token(far, NP - NX + k), NP + k, store)
                rows = [combine(z)]
                for k in range(NX):
                    lane = NP + k
                    rows.append(pack_row(piece_m[:, lane:lane + 1], piece_s[:, lane:lane + 1],
                                         piece_t[:, lane:lane + 1]))
                sub = iota((8, 128), 0)
                tile = jnp.zeros((8, 128), F32)
                for k, row in enumerate(rows):
                    tile = jnp.where(sub == k, row, tile)
                msg_src[...] = tile

            @pl.when(t == XSTEP + 1)
            def _():
                msg_copy.start()

            return ()

        lax.fori_loop(0, last, step, ())
        for k in range(NX):
            x_copy(k).start()
        for k in range(RING):
            outer_copy(last - RING + k).wait_send()
        msg_copy.wait_send()

    @pl.when(inner)
    def _():
        def step(t, _):
            i, ph = lax.rem(t, NP), t // NP
            g = t - LAG
            far_copy(far_in.at[t], t, far_in, far_recv).wait_recv()

            @pl.when((t >= 1) & (t <= 2 * NP))
            def _():
                @pl.when(t - 1 >= RING)
                def _():
                    inner_copy(t - 1 - RING).wait_send()
                inner_copy(t - 1).start()

            @pl.when((g >= 1) & (g <= NP))
            def _():
                @pl.when(g - 1 >= RING)
                def _():
                    near_copy(g - 1 - RING).wait_send()
                near_copy(g - 1).start()

            for k in range(NX):
                @pl.when(g - 1 == 2 * NP - NX + k)
                def _(k=k):
                    x_part_copy(k).start()

            @pl.when(t < 2 * NP)
            def _():
                far_in[t] = far_in[t] + part[(3 - ph) * NP + i]

            @pl.when((g >= 0) & (g < 2 * NP))
            def _():
                far_copy(far_in.at[g], g, side_in, side_recv).wait_recv()

                @pl.when((g < NP) | (g >= 2 * NP - NX))
                def _():
                    side_in[g] = side_in[g] + part[g]

            @pl.when(t < NP)
            def _():
                products(i)

            @pl.when(t >= 2 * NP)
            def _():
                finish(part[NP + i] + side_in[NP + i] + far_in[t], first_token(z, i), i, out_store(i))

            return ()

        lax.fori_loop(0, last, step, ())
        msg_copy.wait_recv()
        msg = msg_in[...]
        for k in range(NX):
            lane = NP - NX + k
            row = msg[k + 1:k + 2]
            put(piece_m, lane, to_col(row))
            put(piece_s, lane, to_col(pltpu.roll(row, 96, 1)))
            put(piece_t, lane, to_col(pltpu.roll(row, 64, 1)))
        mine = combine(z)
        theirs = msg[0:1]
        sub, lane = iota((8, 128), 0), iota((8, 128), 1)
        tile = jnp.where(sub == 0, jnp.where(z == 1, theirs, mine),
                         jnp.where(sub == 1, jnp.where(z == 1, mine, theirs), jnp.where(lane < 32, mine, 0.0)))
        stats[2 * v + z - 1] = tile

    def st_copy(slot, dz, dv):
        return pltpu.make_async_remote_copy(src_ref=stats.at[slot], dst_ref=stats.at[slot],
                                            send_sem=st_send.at[4 * dv + dz], recv_sem=st_recv.at[slot],
                                            device_id={"hid": lax.rem(z + dz, 4), "vocab": lax.rem(v + dv, 4)},
                                            device_id_type=MESH)

    peers = [(dz, dv) for dv in range(4) for dz in range(4) if dv or dz]

    @pl.when(inner)
    def _():
        for dz, dv in peers:
            st_copy(2 * v + z - 1, dz, dv).start()
        for k in range(RING):
            inner_copy(2 * NP - RING + k).wait_send()
            near_copy(NP - RING + k).wait_send()
        for k in range(NX):
            x_part_copy(k).wait_send()

    for slot in range(8):
        @pl.when(outer | (2 * v + z - 1 != slot))
        def _(slot=slot):
            st_copy(slot, 1, 0).wait_recv()

    table = stats[...].reshape(64, 128)
    row_id = iota((64, 128), 0)
    m_row = jnp.max(table, axis=0, keepdims=True)
    scale = jnp.exp(table - m_row)
    live = (row_id & 7) < 2
    tot = jnp.where(live, pltpu.roll(table, 96, 1) * scale, 0.0)
    t_val = jnp.where(live, pltpu.roll(table, 64, 1) * scale, 0.0)
    s_row = jnp.sum(tot, axis=0, keepdims=True)
    me = v * 16 + (z // 2) * 8 + lax.rem(z, 2)
    below_row = jnp.sum(jnp.where(row_id < me, tot, 0.0), axis=0, keepdims=True)

    low = (((row_id >> 3) * 2 + (row_id & 7)) * cols).astype(F32)
    tgt_lanes = jnp.sum(jnp.where(iota((32, 128), 0) == iota((32, 128), 1), tgt, 0.0), axis=0, keepdims=True)
    at_tgt = jnp.sum(jnp.where(low + float(cols) <= tgt_lanes, tot, jnp.where(low <= tgt_lanes, t_val, 0.0)),
                     axis=0, keepdims=True)
    tgt_out_ref[...] = (at_tgt / s_row)[:, 0:32]

    m_col, s_col, below = to_col(m_row), to_col(s_row), to_col(below_row)
    alive = iota((32, 128), 1) < NP
    mult = jnp.exp(jnp.where(alive, piece_m[...], m_col) - m_col)
    totals = jnp.where(alive, piece_s[...] * mult, 0.0)
    shift = (below + (scan_lanes(totals) - totals)) / s_col
    mult = mult / s_col

    def spread(i, src):
        out_ref[:, i * tok:(i + 1) * tok] = src * mult[:, i:i + 1] + shift[:, i:i + 1]

    for i in range(NP - NX):
        spread(i, out_ref[:, i * tok:(i + 1) * tok])

    @pl.when(outer)
    def _():
        for i in range(NP - NX, NP):
            spread(i, out_ref[:, i * tok:(i + 1) * tok])
        for k in range(NX):
            x_copy(k).wait_send()

    @pl.when(inner)
    def _():
        for k in range(NX):
            x_copy(k).wait_recv()
            spread(NP - NX + k, x_in[k])
        for dz, dv in peers:
            st_copy(2 * v + z - 1, dz, dv).wait_send()


def solution(mesh):
    assert mesh.shape["hid"] == 4 and mesh.shape["vocab"] == 4

    def local_step(h_blk, w_blk, temp_blk, tgt_blk):
        rows, depth = h_blk.shape
        cols = w_blk.shape[1] // 4
        tok = cols // NP
        assert rows == 32 and tok % 128 == 0
        block = (rows, tok)
        vmem, dma = pltpu.VMEM, pltpu.SemaphoreType.DMA
        any_space = pl.BlockSpec(memory_space=pltpu.MemorySpace.HBM)
        in_vmem = pl.BlockSpec(memory_space=pltpu.VMEM)
        table, at_tgt = pl.pallas_call(
            functools.partial(kernel, tok),
            out_shape=(jax.ShapeDtypeStruct((rows, cols), F32), jax.ShapeDtypeStruct((1, rows), F32)),
            in_specs=[any_space, any_space, in_vmem, in_vmem],
            out_specs=(in_vmem, in_vmem),
            scratch_shapes=[
                vmem((rows, depth), BF16),
                vmem((4, depth, tok), BF16),
                vmem((4 * NP, *block), F32),
                vmem((3 * NP, *block), F32),
                vmem((2 * NP, *block), F32),
                vmem((NP, *block), F32),
                vmem((NX, *block), F32),
                vmem((NX, *block), F32),
                vmem((NX, *block), F32),
                vmem((32, 128), F32),
                vmem((32, 128), F32),
                vmem((32, 128), F32),
                vmem((8, 128), F32),
                vmem((8, 128), F32),
                vmem((8, 8, 128), F32),
                dma, dma((4,)),
                dma((RING,)), dma((3 * NP,)), dma((2 * NP,)),
                dma((RING,)), dma((NP,)),
                dma((NX,)), dma((NX,)), dma((NX,)), dma((NX,)),
                dma, dma, dma((16,)), dma((8,)),
            ],
            compiler_params=pltpu.CompilerParams(collective_id=0, has_side_effects=True,
                                                 vmem_limit_bytes=48 * 2 ** 20),
            name="head_cdf",
        )(h_blk, w_blk, temp_blk.reshape(1, rows), tgt_blk.reshape(1, rows))
        return table, at_tgt.reshape(rows)

    return jax.shard_map(local_step, mesh=mesh,
                         in_specs=(P("data", "hid"), P("hid", "vocab"), P("data"), P("data")),
                         out_specs=(P("data", ("vocab", "hid")), P("data")), check_vma=False)
```

time: 307 us -> 151 us (0.49)
  Pallas kernels: 0 us -> 143 us
  waiting for transfers between devices: 142 us -> 0 us
  blocking collectives: 105 us -> 0 us
  matrix products: 18.8 us -> 0 us
  between operations: 15.5 us -> 0.65 us
  other arithmetic: 9.4 us -> 0 us
  local copies, waits for them, and re-layouts: 10.8 us -> 3.87 us
    pallas_call x0 -> x1, Pallas kernels: none -> 143 us  [local_step(): pl.pallas_call(functools.partial(kernel, tok), out_shape=(jax.ShapeDtypeS...]
    reduce_scatter x1 -> x0, waiting for transfers between devices: 142 us -> none  [local_step(): lax.psum_scatter(part_logits, 'hid', scatter_dimension=1, tiled=True)]
    psum x2 -> x0, blocking collectives: 59.8 us -> none  [the longest x1 30.1 us: local_step(): cdf_tgt = lax.psum(jnp.where(in_range, picked, 0.0), ('vocab', 'hid'))]
    pmax x1 -> x0, blocking collectives: 29.2 us -> none  [local_step(): glob_max = lax.pmax(jnp.max(logits, axis=1), ('vocab', 'hid'))]
    dot_general x1 -> x0, matrix products: 18.8 us -> none  [local_step(): part_logits = jnp.dot(h_blk, w_blk, preferred_element_type=jnp.float32)]
    unnamed x2 -> x0, blocking collectives: 16.3 us -> none
    another operation x4 -> x0, local copies, waits for them, and re-layouts: 4.01 us -> none
    another operation x3 -> x0, other arithmetic: 3.6 us -> none
  transfers between devices with their start and end apart: 1 -> 0, of which waited for: 1 -> 0; matrix products, arithmetic and copies ran while one was open for 0% -> 0% of each run, Pallas kernels for 0% -> 0%
where the time goes in v1:
time: 151 us; the launch traced here: 148 us
  Pallas kernels  143 us (95%)
  local copies, waits for them, and re-layouts  3.87 us (3%)
    pallas_call x1, Pallas kernels, local_step(): pl.pallas_call(functools.partial(kernel, tok), out_shape=(jax.ShapeDtypeS...  143 us
    unnamed x8, local copies, waits for them, and re-layouts  3.87 us

profile of v1, /device:TPU:16, one launch (start us, length us, event | category | flops | bytes accessed | tf_op | source)
XLA Modules:
  0.0 147.8 jit_solution(3311559443944892846)
XLA Ops:
  0.6 0.0 copy-start
  0.6 0.7 copy-done
  1.4 0.0 copy-start.1
  1.4 0.7 copy-done.1
  2.0 0.0 copy-start.2
  2.0 0.7 copy-done.2
  2.7 143.3 %head_cdf.1 = (f32[32,16384]{1,0:T(8,128)S(1)}, f32[1,32]{1,0:T(1,128)S(1)}) custom-call(bf16[32,288]{1,0:T(8,128)(2,1)S(1)} %copy-done, bf16[288,65536]{1,0:T(8,128)(2,1)} %w_hbm.1, f32[1,32]{1,0:T(1,128)S(1)} %bitcast.3, s32[1,32]{1,0:T(1,128)S(1)} %bitcast.4), custom_call_target="tpu_custom_call" | custom-call | tf_op jit(solution)/shard_map/head_cdf/pallas_call | solution.py:376
  145.9 1.3 copy.8
  147.3 0.5 copy.9
Async XLA Ops:
  0.6 0.7 copy-start
  1.4 0.7 copy-start.1
  2.0 0.7 copy-start.2

commit v2 on v1

--- a/solution.py
+++ b/solution.py
@@ -9,10 +9,11 @@
 
 MESH = pl.DeviceIdType.MESH
 NP = 16
-NX = 2
-RING = 4
-LAG = 2
-XSTEP = 2 * NP + 4
+NX = 4
+RING = 3
+LAG = 3
+XSTEP = 2 * NP + 5
+VMEM_LIMIT = 67043328 - 2 ** 21 - 2 ** 13
 F32 = jnp.float32
 BF16 = jnp.bfloat16
 
@@ -32,11 +33,11 @@
     return jnp.sum(picked, axis=0, keepdims=True)
 
 
-def kernel(tok, h_hbm, w_hbm, temp_ref, tgt_ref, out_ref, tgt_out_ref,
-           h_buf, w_buf, part, far_in, side_in, near_in, x_part, x_src, x_in, piece_m, piece_s, piece_t,
-           msg_src, msg_in, stats,
-           h_sem, w_sem, far_send, far_recv, side_recv, near_send, near_recv, xp_send, xp_recv, x_send, x_recv,
-           msg_send, msg_recv, st_send, st_recv):
+def kernel(tok, h_hbm, w_hbm, temp_hbm, tgt_hbm, out_ref, tgt_out_ref,
+           h_buf, temp_buf, tgt_buf, w_buf, part, far_in, side_in, near_in, x_part, x_src, x_in, piece_m, piece_s, piece_t,
+           msg_src, msg_in, stats, res_src, res_in,
+           h_sem, temp_sem, tgt_sem, w_sem, far_send, far_recv, side_recv, near_send, near_recv, xp_send, xp_recv, x_send, x_recv,
+           msg_send, msg_recv, st_send, st_recv, res_send, res_recv, ready):
     z, v = lax.axis_index("hid"), lax.axis_index("vocab")
     outer = (z == 0) | (z == 3)
     inner = (z == 1) | (z == 2)
@@ -51,16 +52,29 @@
         return pltpu.make_async_copy(w_hbm.at[:, pl.ds(start, tok)], w_buf.at[slot], w_sem.at[slot])
 
     h_copy = pltpu.make_async_copy(h_hbm, h_buf, h_sem)
+    temp_copy = pltpu.make_async_copy(temp_hbm, temp_buf, temp_sem)
+    tgt_copy = pltpu.make_async_copy(tgt_hbm, tgt_buf, tgt_sem)
+    barrier = pltpu.get_barrier_semaphore()
+
+    def greet(dev):
+        pl.semaphore_signal(barrier, inc=1, device_id=dev, device_id_type=MESH)
+
+    greet({"hid": far})
+
+    @pl.when(inner)
+    def _():
+        greet({"hid": near})
+
     h_copy.start()
-    for slot, rel in enumerate((3, 0, 2, 1)):
-        w_load(rel, 0, slot).start()
-
-    barrier = pltpu.get_barrier_semaphore()
-    for dv in range(4):
-        for dz in range(4):
-            if dv or dz:
-                pl.semaphore_signal(barrier, inc=1, device_id={"hid": lax.rem(z + dz, 4), "vocab": lax.rem(v + dv, 4)},
-                                    device_id_type=MESH)
+    w_load(3, 0, 0).start()
+
+    @pl.when(inner)
+    def _():
+        for dv in range(1, 4):
+            greet({"vocab": lax.rem(v + dv, 4)})
+
+    temp_copy.start()
+    tgt_copy.start()
 
     def product(rel, i, slot):
         w_load(rel, i, slot).wait()
@@ -83,9 +97,6 @@
     piece_m[...] = jnp.zeros_like(piece_m)
     piece_s[...] = jnp.zeros_like(piece_s)
     piece_t[...] = jnp.zeros_like(piece_t)
-    temp = to_col(temp_ref[...])
-    tgt_row = tgt_ref[...].astype(F32)
-    tgt = to_col(tgt_row)
 
     def put(ref, lane, value):
         ref[...] = jnp.where(iota((32, 128), 1) == lane, value, ref[...])
@@ -170,7 +181,21 @@
 
     h_copy.wait()
     product(3, 0, 0)
-    pl.semaphore_wait(barrier, 15)
+    for slot, rel in ((1, 0), (2, 2), (3, 1)):
+        w_load(rel, 0, slot).start()
+    temp_copy.wait()
+    tgt_copy.wait()
+    temp = to_col(temp_buf[...])
+    tgt = to_col(tgt_buf[...].astype(F32))
+
+    @pl.when(outer)
+    def _():
+        pl.semaphore_wait(barrier, 1)
+
+    @pl.when(inner)
+    def _():
+        pl.semaphore_wait(barrier, 5)
+        pl.semaphore_signal(ready, inc=1, device_id={"hid": far}, device_id_type=MESH)
 
     def out_store(i):
         def store(b, c):
@@ -292,73 +317,94 @@
                          jnp.where(sub == 1, jnp.where(z == 1, mine, theirs), jnp.where(lane < 32, mine, 0.0)))
         stats[2 * v + z - 1] = tile
 
-    def st_copy(slot, dz, dv):
+    slot = 2 * v + z - 1
+
+    def st_copy(slot, cross, dv):
         return pltpu.make_async_remote_copy(src_ref=stats.at[slot], dst_ref=stats.at[slot],
-                                            send_sem=st_send.at[4 * dv + dz], recv_sem=st_recv.at[slot],
-                                            device_id={"hid": lax.rem(z + dz, 4), "vocab": lax.rem(v + dv, 4)},
+                                            send_sem=st_send.at[4 * cross + dv], recv_sem=st_recv.at[slot],
+                                            device_id={"hid": far if cross else z, "vocab": lax.rem(v + dv, 4)},
                                             device_id_type=MESH)
 
-    peers = [(dz, dv) for dv in range(4) for dz in range(4) if dv or dz]
+    peers = [(cross, dv) for cross in (1, 0) for dv in range(4) if cross or dv]
+    res_copy = pltpu.make_async_remote_copy(src_ref=res_src, dst_ref=res_in, send_sem=res_send, recv_sem=res_recv,
+                                            device_id={"hid": near}, device_id_type=MESH)
+
+    def settle(m_row, s_row, below_row):
+        m_col, s_col, below = to_col(m_row), to_col(s_row), to_col(below_row)
+        alive = iota((32, 128), 1) < NP
+        mult = jnp.exp(jnp.where(alive, piece_m[...], m_col) - m_col)
+        totals = jnp.where(alive, piece_s[...] * mult, 0.0)
+        return mult / s_col, (below + (scan_lanes(totals) - totals)) / s_col
+
+    def spread(i, src, mult, shift):
+        out_ref[:, i * tok:(i + 1) * tok] = src * mult[:, i:i + 1] + shift[:, i:i + 1]
 
     @pl.when(inner)
     def _():
-        for dz, dv in peers:
-            st_copy(2 * v + z - 1, dz, dv).start()
+        pl.semaphore_wait(ready, 1)
+        for cross, dv in peers:
+            st_copy(slot, cross, dv).start()
         for k in range(RING):
             inner_copy(2 * NP - RING + k).wait_send()
             near_copy(NP - RING + k).wait_send()
         for k in range(NX):
             x_part_copy(k).wait_send()
-
-    for slot in range(8):
-        @pl.when(outer | (2 * v + z - 1 != slot))
-        def _(slot=slot):
-            st_copy(slot, 1, 0).wait_recv()
-
-    table = stats[...].reshape(64, 128)
-    row_id = iota((64, 128), 0)
-    m_row = jnp.max(table, axis=0, keepdims=True)
-    scale = jnp.exp(table - m_row)
-    live = (row_id & 7) < 2
-    tot = jnp.where(live, pltpu.roll(table, 96, 1) * scale, 0.0)
-    t_val = jnp.where(live, pltpu.roll(table, 64, 1) * scale, 0.0)
-    s_row = jnp.sum(tot, axis=0, keepdims=True)
-    me = v * 16 + (z // 2) * 8 + lax.rem(z, 2)
-    below_row = jnp.sum(jnp.where(row_id < me, tot, 0.0), axis=0, keepdims=True)
-
-    low = (((row_id >> 3) * 2 + (row_id & 7)) * cols).astype(F32)
-    tgt_lanes = jnp.sum(jnp.where(iota((32, 128), 0) == iota((32, 128), 1), tgt, 0.0), axis=0, keepdims=True)
-    at_tgt = jnp.sum(jnp.where(low + float(cols) <= tgt_lanes, tot, jnp.where(low <= tgt_lanes, t_val, 0.0)),
-                     axis=0, keepdims=True)
-    tgt_out_ref[...] = (at_tgt / s_row)[:, 0:32]
-
-    m_col, s_col, below = to_col(m_row), to_col(s_row), to_col(below_row)
-    alive = iota((32, 128), 1) < NP
-    mult = jnp.exp(jnp.where(alive, piece_m[...], m_col) - m_col)
-    totals = jnp.where(alive, piece_s[...] * mult, 0.0)
-    shift = (below + (scan_lanes(totals) - totals)) / s_col
-    mult = mult / s_col
-
-    def spread(i, src):
-        out_ref[:, i * tok:(i + 1) * tok] = src * mult[:, i:i + 1] + shift[:, i:i + 1]
-
-    for i in range(NP - NX):
-        spread(i, out_ref[:, i * tok:(i + 1) * tok])
+        for other in range(8):
+            @pl.when(slot != other)
+            def _(other=other):
+                st_copy(other, 0, 1).wait_recv()
+
+        table = stats[...].reshape(64, 128)
+        row_id = iota((64, 128), 0)
+        m_row = jnp.max(table, axis=0, keepdims=True)
+        scale = jnp.exp(table - m_row)
+        live = (row_id & 7) < 2
+        tot = jnp.where(live, pltpu.roll(table, 96, 1) * scale, 0.0)
+        t_val = jnp.where(live, pltpu.roll(table, 64, 1) * scale, 0.0)
+        s_row = jnp.sum(tot, axis=0, keepdims=True)
+
+        def below(zz):
+            me = v * 16 + (zz // 2) * 8 + lax.rem(zz, 2)
+            return jnp.sum(jnp.where(row_id < me, tot, 0.0), axis=0, keepdims=True)
+
+        low = (((row_id >> 3) * 2 + (row_id & 7)) * cols).astype(F32)
+        tgt_lanes = jnp.sum(jnp.where(iota((32, 128), 0) == iota((32, 128), 1), tgt, 0.0), axis=0, keepdims=True)
+        at_tgt = jnp.sum(jnp.where(low + float(cols) <= tgt_lanes, tot, jnp.where(low <= tgt_lanes, t_val, 0.0)),
+                         axis=0, keepdims=True) / s_row
+        sub = iota((8, 128), 0)
+        res_src[...] = jnp.where(sub == 0, m_row, jnp.where(sub == 1, s_row, jnp.where(sub == 2, below(near), at_tgt)))
+        tgt_out_ref[...] = at_tgt[:, 0:32]
+        mult, shift = settle(m_row, s_row, below(z))
+        res_copy.start()
+        for i in range(NP - NX):
+            spread(i, out_ref[:, i * tok:(i + 1) * tok], mult, shift)
+        for k in range(NX):
+            x_copy(k).wait_recv()
+            spread(NP - NX + k, x_in[k], mult, shift)
+        for cross, dv in peers:
+            st_copy(slot, cross, dv).wait_send()
+        res_copy.wait_send()
 
     @pl.when(outer)
     def _():
-        for i in range(NP - NX, NP):
-            spread(i, out_ref[:, i * tok:(i + 1) * tok])
+        res_copy.wait_recv()
+        res = res_in[...]
+        tgt_out_ref[...] = res[3:4, 0:32]
+        mult, shift = settle(res[0:1], res[1:2], res[2:3])
+        for i in range(NP):
+            spread(i, out_ref[:, i * tok:(i + 1) * tok], mult, shift)
         for k in range(NX):
             x_copy(k).wait_send()
 
-    @pl.when(inner)
-    def _():
-        for k in range(NX):
-            x_copy(k).wait_recv()
-            spread(NP - NX + k, x_in[k])
-        for dz, dv in peers:
-            st_copy(2 * v + z - 1, dz, dv).wait_send()
+
+def write_kernel(table_ref, at_tgt_ref, table_hbm, at_tgt_hbm, sems, at_sem):
+    copies = [pltpu.make_async_copy(table_ref.at[pl.ds(8 * k, 8)], table_hbm.at[pl.ds(8 * k, 8)], sems.at[k])
+              for k in range(4)]
+    copies.append(pltpu.make_async_copy(at_tgt_ref, at_tgt_hbm, at_sem))
+    for c in copies:
+        c.start()
+    for c in copies:
+        c.wait()
 
 
 def solution(mesh):
@@ -371,15 +417,16 @@
         assert rows == 32 and tok % 128 == 0
         block = (rows, tok)
         vmem, dma = pltpu.VMEM, pltpu.SemaphoreType.DMA
-        any_space = pl.BlockSpec(memory_space=pltpu.MemorySpace.HBM)
+        hbm = pl.BlockSpec(memory_space=pltpu.MemorySpace.HBM)
         in_vmem = pl.BlockSpec(memory_space=pltpu.VMEM)
+        shapes = (jax.ShapeDtypeStruct((rows, cols), F32), jax.ShapeDtypeStruct((1, rows), F32))
         table, at_tgt = pl.pallas_call(
             functools.partial(kernel, tok),
-            out_shape=(jax.ShapeDtypeStruct((rows, cols), F32), jax.ShapeDtypeStruct((1, rows), F32)),
-            in_specs=[any_space, any_space, in_vmem, in_vmem],
+            out_shape=(pltpu.VMEM((rows, cols), F32), pltpu.VMEM((1, rows), F32)),
+            in_specs=[hbm] * 4,
             out_specs=(in_vmem, in_vmem),
             scratch_shapes=[
-                vmem((rows, depth), BF16),
+                vmem((rows, depth), BF16), vmem((1, rows), F32), vmem((1, rows), jnp.int32),
                 vmem((4, depth, tok), BF16),
                 vmem((4 * NP, *block), F32),
                 vmem((3 * NP, *block), F32),
@@ -391,19 +438,26 @@
                 vmem((32, 128), F32),
                 vmem((32, 128), F32),
                 vmem((32, 128), F32),
-                vmem((8, 128), F32),
-                vmem((8, 128), F32),
-                vmem((8, 8, 128), F32),
-                dma, dma((4,)),
+                vmem((8, 128), F32), vmem((8, 128), F32), vmem((8, 8, 128), F32),
+                vmem((8, 128), F32), vmem((8, 128), F32),
+                dma, dma, dma, dma((4,)),
                 dma((RING,)), dma((3 * NP,)), dma((2 * NP,)),
                 dma((RING,)), dma((NP,)),
                 dma((NX,)), dma((NX,)), dma((NX,)), dma((NX,)),
-                dma, dma, dma((16,)), dma((8,)),
+                dma, dma, dma((8,)), dma((8,)), dma, dma, pltpu.SemaphoreType.REGULAR,
             ],
-            compiler_params=pltpu.CompilerParams(collective_id=0, has_side_effects=True,
-                                                 vmem_limit_bytes=48 * 2 ** 20),
+            compiler_params=pltpu.CompilerParams(collective_id=0, has_side_effects=True, vmem_limit_bytes=VMEM_LIMIT),
             name="head_cdf",
         )(h_blk, w_blk, temp_blk.reshape(1, rows), tgt_blk.reshape(1, rows))
+        table, at_tgt = pl.pallas_call(
+            write_kernel,
+            out_shape=shapes,
+            in_specs=[in_vmem, in_vmem],
+            out_specs=(hbm, hbm),
+            scratch_shapes=[dma((4,)), dma],
+            compiler_params=pltpu.CompilerParams(vmem_limit_bytes=2 ** 20),
+            name="write",
+        )(table, at_tgt)
         return table, at_tgt.reshape(rows)
 
     return jax.shard_map(local_step, mesh=mesh,

time: 151 us -> 145 us (0.960)
  local copies, waits for them, and re-layouts: 3.87 us -> 0 us
    unnamed x8 -> x0, local copies, waits for them, and re-layouts: 3.87 us -> none
    pallas_call x1 -> x2, Pallas kernels: 143 us -> 142 us  [the longest x1 141 us: local_step(): pl.pallas_call(functools.partial(kernel, tok), out_shape=(pltpu.VMEM((row...]
where the time goes in v2:
time: 145 us; the launch traced here: 143 us
  Pallas kernels  142 us (98%)
    pallas_call x1, Pallas kernels, local_step(): pl.pallas_call(functools.partial(kernel, tok), out_shape=(pltpu.VMEM((row...  141 us

profile of v2, /device:TPU:16, one launch (start us, length us, event | category | flops | bytes accessed | tf_op | source)
XLA Modules:
  0.0 142.8 jit_solution(6178535890428661768)
XLA Ops:
  0.6 140.8 %head_cdf.1 = (f32[32,16384]{1,0:T(8,128)S(1)}, f32[1,32]{1,0:T(1,128)S(1)}) custom-call(bf16[32,288]{1,0:T(8,128)(2,1)} %h_hbm.1, bf16[288,65536]{1,0:T(8,128)(2,1)} %w_hbm.1, f32[1,32]{1,0:T(1,128)} %bitcast.3, s32[1,32]{1,0:T(1,128)} %bitcast.4), custom_call_target="tpu_custom_call" | custom-call | tf_op jit(solution)/shard_map/head_cdf/pallas_call | solution.py:423
  141.5 1.4 write.1

commit v3 on v2

--- a/solution.py
+++ b/solution.py
@@ -9,10 +9,11 @@
 
 MESH = pl.DeviceIdType.MESH
 NP = 16
-NX = 4
-RING = 3
-LAG = 3
-XSTEP = 2 * NP + 5
+NX = 6
+RING = 4
+LAG = 4
+XSTEP = 2 * NP - 3
+SUB = 2
 VMEM_LIMIT = 67043328 - 2 ** 21 - 2 ** 13
 F32 = jnp.float32
 BF16 = jnp.bfloat16
@@ -36,7 +37,7 @@
 def kernel(tok, h_hbm, w_hbm, temp_hbm, tgt_hbm, out_ref, tgt_out_ref,
            h_buf, temp_buf, tgt_buf, w_buf, part, far_in, side_in, near_in, x_part, x_src, x_in, piece_m, piece_s, piece_t,
            msg_src, msg_in, stats, res_src, res_in,
-           h_sem, temp_sem, tgt_sem, w_sem, far_send, far_recv, side_recv, near_send, near_recv, xp_send, xp_recv, x_send, x_recv,
+           h_sem, temp_sem, tgt_sem, w_sem, sub_w, sub_send, sub_recv, far_send, far_recv, side_recv, near_send, near_recv, xp_send, xp_recv, x_send, x_recv,
            msg_send, msg_recv, st_send, st_recv, res_send, res_recv, ready):
     z, v = lax.axis_index("hid"), lax.axis_index("vocab")
     outer = (z == 0) | (z == 3)
@@ -44,6 +45,7 @@
     far = jnp.where(z < 2, z + 1, z - 1)
     near = jnp.where(z == 1, 0, 3)
     cols = NP * tok
+    part_tok = tok // SUB
     last = 3 * NP - NX
 
     def w_load(rel, i, slot):
@@ -59,14 +61,22 @@
     def greet(dev):
         pl.semaphore_signal(barrier, inc=1, device_id=dev, device_id_type=MESH)
 
+    def part_of(k):
+        return pl.ds(k * part_tok, part_tok)
+
+    def sub_load(k):
+        owner = jnp.where(z < 2, 3, 0)
+        start = pl.multiple_of(owner * cols + k * part_tok, part_tok)
+        return pltpu.make_async_copy(w_hbm.at[:, pl.ds(start, part_tok)], w_buf.at[0, :, part_of(k)], sub_w.at[k])
+
+    @pl.when(inner)
+    def _():
+        greet({"hid": near})
+
+    h_copy.start()
+    for k in range(SUB):
+        sub_load(k).start()
     greet({"hid": far})
-
-    @pl.when(inner)
-    def _():
-        greet({"hid": near})
-
-    h_copy.start()
-    w_load(3, 0, 0).start()
 
     @pl.when(inner)
     def _():
@@ -92,6 +102,15 @@
         @pl.when(i + 1 < NP)
         def _():
             product(3, i + 1, 0)
+
+    def sub_product(k):
+        sub_load(k).wait()
+        part[3 * NP, :, part_of(k)] = jnp.dot(h_buf[...], w_buf[0, :, part_of(k)], preferred_element_type=F32)
+
+    def sub_copy(k):
+        return pltpu.make_async_remote_copy(src_ref=part.at[3 * NP, :, part_of(k)], dst_ref=far_in.at[0, :, part_of(k)],
+                                            send_sem=sub_send.at[k], recv_sem=sub_recv.at[k],
+                                            device_id={"hid": far}, device_id_type=MESH)
 
     tri = (iota((128, 128), 0) <= iota((128, 128), 1)).astype(BF16)
     piece_m[...] = jnp.zeros_like(piece_m)
@@ -155,9 +174,12 @@
         return pltpu.make_async_remote_copy(src_ref=src, dst_ref=dst.at[t], send_sem=far_send.at[lax.rem(t, RING)],
                                             recv_sem=sems.at[t], device_id={"hid": far}, device_id_type=MESH)
 
+    def part_index(t):
+        i, ph = lax.rem(t, NP), t // NP
+        return (3 - ph) * NP + jnp.where(ph == 1, lax.rem(i + NP - NX, NP), i)
+
     def outer_copy(t):
-        i, ph = lax.rem(t, NP), t // NP
-        return far_copy(part.at[(3 - ph) * NP + i], t, far_in, far_recv)
+        return far_copy(part.at[part_index(t)], t, far_in, far_recv)
 
     def inner_copy(t):
         return far_copy(far_in.at[t], t, side_in, side_recv)
@@ -168,7 +190,7 @@
                                             device_id={"hid": near}, device_id_type=MESH)
 
     def x_part_copy(k):
-        return pltpu.make_async_remote_copy(src_ref=side_in.at[2 * NP - NX + k], dst_ref=x_part.at[k],
+        return pltpu.make_async_remote_copy(src_ref=side_in.at[NP + k], dst_ref=x_part.at[k],
                                             send_sem=xp_send.at[k], recv_sem=xp_recv.at[k],
                                             device_id={"hid": near}, device_id_type=MESH)
 
@@ -180,18 +202,26 @@
                                             device_id={"hid": far}, device_id_type=MESH)
 
     h_copy.wait()
-    product(3, 0, 0)
-    for slot, rel in ((1, 0), (2, 2), (3, 1)):
-        w_load(rel, 0, slot).start()
+    for k in range(SUB):
+        sub_product(k)
+        if k == 0:
+            for slot, rel in ((1, 0), (2, 2), (3, 1)):
+                w_load(rel, 0, slot).start()
+
+            @pl.when(outer)
+            def _():
+                pl.semaphore_wait(barrier, 1)
+
+        @pl.when(outer)
+        def _(k=k):
+            sub_copy(k).start()
+
+    w_load(3, 1, 0).start()
     temp_copy.wait()
     tgt_copy.wait()
     temp = to_col(temp_buf[...])
     tgt = to_col(tgt_buf[...].astype(F32))
 
-    @pl.when(outer)
-    def _():
-        pl.semaphore_wait(barrier, 1)
-
     @pl.when(inner)
     def _():
         pl.semaphore_wait(barrier, 5)
@@ -207,11 +237,13 @@
         def step(t, _):
             i = lax.rem(t, NP)
 
-            @pl.when(t >= RING)
+            @pl.when(t > RING)
             def _():
                 outer_copy(t - RING).wait_send()
 
-            outer_copy(t).start()
+            @pl.when(t > 0)
+            def _():
+                outer_copy(t).start()
 
             @pl.when(t < NP)
             def _():
@@ -222,25 +254,26 @@
                 near_copy(i).wait_recv()
                 finish(part[i] + near_in[i], first_token(z, i), i, out_store(i))
 
-            @pl.when(t == XSTEP)
-            def _():
-                for k in range(NX):
-                    def store(b, c, k=k):
-                        x_src[k, :, b * 128:(b + 1) * 128] = c
-                    x_part_copy(k).wait_recv()
-                    finish(part[2 * NP - NX + k] + x_part[k], first_token(far, NP - NX + k), NP + k, store)
-                rows = [combine(z)]
+            @pl.when((t >= XSTEP) & (t < XSTEP + NX))
+            def _():
+                k = t - XSTEP
+
+                def store(b, c):
+                    x_src[k, :, b * 128:(b + 1) * 128] = c
+                x_part_copy(k).wait_recv()
+                finish(part[2 * NP - NX + k] + x_part[k], first_token(far, NP - NX + k), NP + k, store)
+
+            @pl.when(t == XSTEP + NX)
+            def _():
+                sub = iota((8, 128), 0)
+                tile = jnp.where(sub == 0, combine(z), 0.0)
                 for k in range(NX):
                     lane = NP + k
-                    rows.append(pack_row(piece_m[:, lane:lane + 1], piece_s[:, lane:lane + 1],
-                                         piece_t[:, lane:lane + 1]))
-                sub = iota((8, 128), 0)
-                tile = jnp.zeros((8, 128), F32)
-                for k, row in enumerate(rows):
-                    tile = jnp.where(sub == k, row, tile)
+                    row = pack_row(piece_m[:, lane:lane + 1], piece_s[:, lane:lane + 1], piece_t[:, lane:lane + 1])
+                    tile = jnp.where(sub == k + 1, row, tile)
                 msg_src[...] = tile
 
-            @pl.when(t == XSTEP + 1)
+            @pl.when(t == XSTEP + NX + 1)
             def _():
                 msg_copy.start()
 
@@ -249,6 +282,8 @@
         lax.fori_loop(0, last, step, ())
         for k in range(NX):
             x_copy(k).start()
+        for k in range(SUB):
+            sub_copy(k).wait_send()
         for k in range(RING):
             outer_copy(last - RING + k).wait_send()
         msg_copy.wait_send()
@@ -256,9 +291,17 @@
     @pl.when(inner)
     def _():
         def step(t, _):
-            i, ph = lax.rem(t, NP), t // NP
+            i = lax.rem(t, NP)
             g = t - LAG
-            far_copy(far_in.at[t], t, far_in, far_recv).wait_recv()
+
+            @pl.when(t == 0)
+            def _():
+                for k in range(SUB):
+                    sub_copy(k).wait_recv()
+
+            @pl.when(t > 0)
+            def _():
+                far_copy(far_in.at[t], t, far_in, far_recv).wait_recv()
 
             @pl.when((t >= 1) & (t <= 2 * NP))
             def _():
@@ -275,21 +318,21 @@
                 near_copy(g - 1).start()
 
             for k in range(NX):
-                @pl.when(g - 1 == 2 * NP - NX + k)
+                @pl.when(g - 1 == NP + k)
                 def _(k=k):
                     x_part_copy(k).start()
 
             @pl.when(t < 2 * NP)
             def _():
-                far_in[t] = far_in[t] + part[(3 - ph) * NP + i]
+                far_in[t] = far_in[t] + part[part_index(t)]
 
             @pl.when((g >= 0) & (g < 2 * NP))
             def _():
                 far_copy(far_in.at[g], g, side_in, side_recv).wait_recv()
 
-                @pl.when((g < NP) | (g >= 2 * NP - NX))
+                @pl.when(g < NP + NX)
                 def _():
-                    side_in[g] = side_in[g] + part[g]
+                    side_in[g] = side_in[g] + part[jnp.where(g < NP, g, g + NP - NX)]
 
             @pl.when(t < NP)
             def _():
@@ -297,7 +340,7 @@
 
             @pl.when(t >= 2 * NP)
             def _():
-                finish(part[NP + i] + side_in[NP + i] + far_in[t], first_token(z, i), i, out_store(i))
+                finish(part[NP + i] + side_in[NP + NX + i] + far_in[t], first_token(z, i), i, out_store(i))
 
             return ()
 
@@ -440,7 +483,7 @@
                 vmem((32, 128), F32),
                 vmem((8, 128), F32), vmem((8, 128), F32), vmem((8, 8, 128), F32),
                 vmem((8, 128), F32), vmem((8, 128), F32),
-                dma, dma, dma, dma((4,)),
+                dma, dma, dma, dma((4,)), dma((SUB,)), dma((SUB,)), dma((SUB,)),
                 dma((RING,)), dma((3 * NP,)), dma((2 * NP,)),
                 dma((RING,)), dma((NP,)),
                 dma((NX,)), dma((NX,)), dma((NX,)), dma((NX,)),

time: 145 us -> 142 us (0.979); the launches traced: 143 us -> 142 us
  no operation moved by 1% of the time
where the time goes in v3:
time: 142 us
  Pallas kernels  141 us (99%)
    pallas_call x1, Pallas kernels, local_step(): pl.pallas_call(functools.partial(kernel, tok), out_shape=(pltpu.VMEM((row...  140 us

profile of v3, /device:TPU:16, one launch (start us, length us, event | category | flops | bytes accessed | tf_op | source)
XLA Modules:
  0.0 141.9 jit_solution(17460798301985417876)
XLA Ops:
  0.6 139.9 %head_cdf.1 = (f32[32,16384]{1,0:T(8,128)S(1)}, f32[1,32]{1,0:T(1,128)S(1)}) custom-call(bf16[32,288]{1,0:T(8,128)(2,1)} %h_hbm.1, bf16[288,65536]{1,0:T(8,128)(2,1)} %w_hbm.1, f32[1,32]{1,0:T(1,128)} %bitcast.3, s32[1,32]{1,0:T(1,128)} %bitcast.4), custom_call_target="tpu_custom_call" | custom-call | tf_op jit(solution)/shard_map/head_cdf/pallas_call | solution.py:466
  140.5 1.4 write.1

commit v4 on v3

--- a/solution.py
+++ b/solution.py
@@ -10,10 +10,11 @@
 MESH = pl.DeviceIdType.MESH
 NP = 16
 NX = 6
-RING = 4
+RING = 2
 LAG = 4
 XSTEP = 2 * NP - 3
 SUB = 2
+AHEAD = 2
 VMEM_LIMIT = 67043328 - 2 ** 21 - 2 ** 13
 F32 = jnp.float32
 BF16 = jnp.bfloat16
@@ -45,10 +46,10 @@
     far = jnp.where(z < 2, z + 1, z - 1)
     near = jnp.where(z == 1, 0, 3)
     cols = NP * tok
-    part_tok = tok // SUB
     last = 3 * NP - NX
 
-    def w_load(rel, i, slot):
+    def w_load(rel, i, lane):
+        slot = lax.rem(i, AHEAD) * 4 + lane
         owner = jnp.where(z < 2, rel, 3 - rel)
         start = pl.multiple_of(owner * cols + i * tok, tok)
         return pltpu.make_async_copy(w_hbm.at[:, pl.ds(start, tok)], w_buf.at[slot], w_sem.at[slot])
@@ -62,12 +63,13 @@
         pl.semaphore_signal(barrier, inc=1, device_id=dev, device_id_type=MESH)
 
     def part_of(k):
-        return pl.ds(k * part_tok, part_tok)
+        return pl.ds(0, tok // 4) if k == 0 else pl.ds(tok // 4, tok - tok // 4)
 
     def sub_load(k):
         owner = jnp.where(z < 2, 3, 0)
-        start = pl.multiple_of(owner * cols + k * part_tok, part_tok)
-        return pltpu.make_async_copy(w_hbm.at[:, pl.ds(start, part_tok)], w_buf.at[0, :, part_of(k)], sub_w.at[k])
+        at = part_of(k)
+        start = pl.multiple_of(owner * cols + at.start, tok // 4)
+        return pltpu.make_async_copy(w_hbm.at[:, pl.ds(start, at.size)], w_buf.at[0, :, at], sub_w.at[k])
 
     @pl.when(inner)
     def _():
@@ -86,13 +88,13 @@
     temp_copy.start()
     tgt_copy.start()
 
-    def product(rel, i, slot):
-        w_load(rel, i, slot).wait()
-        part[rel * NP + i] = jnp.dot(h_buf[...], w_buf[slot], preferred_element_type=F32)
-
-        @pl.when(i + 1 < NP)
+    def product(rel, i, lane):
+        w_load(rel, i, lane).wait()
+        part[rel * NP + i] = jnp.dot(h_buf[...], w_buf[lax.rem(i, AHEAD) * 4 + lane], preferred_element_type=F32)
+
+        @pl.when(i + AHEAD < NP)
         def _():
-            w_load(rel, i + 1, slot).start()
+            w_load(rel, i + AHEAD, lane).start()
 
     def products(i):
         product(0, i, 1)
@@ -205,8 +207,10 @@
     for k in range(SUB):
         sub_product(k)
         if k == 0:
-            for slot, rel in ((1, 0), (2, 2), (3, 1)):
-                w_load(rel, 0, slot).start()
+            for i in range(AHEAD):
+                for lane, rel in ((0, 3), (1, 0), (2, 2), (3, 1)):
+                    if i or lane:
+                        w_load(rel, i, lane).start()
 
             @pl.when(outer)
             def _():
@@ -216,7 +220,7 @@
         def _(k=k):
             sub_copy(k).start()
 
-    w_load(3, 1, 0).start()
+    w_load(3, AHEAD, 0).start()
     temp_copy.wait()
     tgt_copy.wait()
     temp = to_col(temp_buf[...])
@@ -440,10 +444,8 @@
             x_copy(k).wait_send()
 
 
-def write_kernel(table_ref, at_tgt_ref, table_hbm, at_tgt_hbm, sems, at_sem):
-    copies = [pltpu.make_async_copy(table_ref.at[pl.ds(8 * k, 8)], table_hbm.at[pl.ds(8 * k, 8)], sems.at[k])
-              for k in range(4)]
-    copies.append(pltpu.make_async_copy(at_tgt_ref, at_tgt_hbm, at_sem))
+def write_kernel(table_ref, at_tgt_ref, table_hbm, at_tgt_hbm, sem, at_sem):
+    copies = (pltpu.make_async_copy(table_ref, table_hbm, sem), pltpu.make_async_copy(at_tgt_ref, at_tgt_hbm, at_sem))
     for c in copies:
         c.start()
     for c in copies:
@@ -470,7 +472,7 @@
             out_specs=(in_vmem, in_vmem),
             scratch_shapes=[
                 vmem((rows, depth), BF16), vmem((1, rows), F32), vmem((1, rows), jnp.int32),
-                vmem((4, depth, tok), BF16),
+                vmem((4 * AHEAD, depth, tok), BF16),
                 vmem((4 * NP, *block), F32),
                 vmem((3 * NP, *block), F32),
                 vmem((2 * NP, *block), F32),
@@ -483,7 +485,7 @@
                 vmem((32, 128), F32),
                 vmem((8, 128), F32), vmem((8, 128), F32), vmem((8, 8, 128), F32),
                 vmem((8, 128), F32), vmem((8, 128), F32),
-                dma, dma, dma, dma((4,)), dma((SUB,)), dma((SUB,)), dma((SUB,)),
+                dma, dma, dma, dma((4 * AHEAD,)), dma((SUB,)), dma((SUB,)), dma((SUB,)),
                 dma((RING,)), dma((3 * NP,)), dma((2 * NP,)),
                 dma((RING,)), dma((NP,)),
                 dma((NX,)), dma((NX,)), dma((NX,)), dma((NX,)),
@@ -497,7 +499,7 @@
             out_shape=shapes,
             in_specs=[in_vmem, in_vmem],
             out_specs=(hbm, hbm),
-            scratch_shapes=[dma((4,)), dma],
+            scratch_shapes=[dma, dma],
             compiler_params=pltpu.CompilerParams(vmem_limit_bytes=2 ** 20),
             name="write",
         )(table, at_tgt)

time: 142 us -> 142 us (level)
  no operation moved by 1% of the time
where the time goes in v4:
time: 142 us
  Pallas kernels  141 us (99%)
    pallas_call x1, Pallas kernels, local_step(): pl.pallas_call(functools.partial(kernel, tok), out_shape=(pltpu.VMEM((row...  140 us

profile of v4, /device:TPU:16, one launch (start us, length us, event | category | flops | bytes accessed | tf_op | source)
XLA Modules:
  0.0 141.8 jit_solution(15305926223707310353)
XLA Ops:
  0.6 139.8 %head_cdf.1 = (f32[32,16384]{1,0:T(8,128)S(1)}, f32[1,32]{1,0:T(1,128)S(1)}) custom-call(bf16[32,288]{1,0:T(8,128)(2,1)} %h_hbm.1, bf16[288,65536]{1,0:T(8,128)(2,1)} %w_hbm.1, f32[1,32]{1,0:T(1,128)} %bitcast.3, s32[1,32]{1,0:T(1,128)} %bitcast.4), custom_call_target="tpu_custom_call" | custom-call | tf_op jit(solution)/shard_map/head_cdf/pallas_call | solution.py:468
  140.5 1.3 write.1

commit v5 on v4

--- a/solution.py
+++ b/solution.py
@@ -13,7 +13,7 @@
 RING = 2
 LAG = 4
 XSTEP = 2 * NP - 3
-SUB = 2
+SUB = 3
 AHEAD = 2
 VMEM_LIMIT = 67043328 - 2 ** 21 - 2 ** 13
 F32 = jnp.float32
@@ -63,12 +63,13 @@
         pl.semaphore_signal(barrier, inc=1, device_id=dev, device_id_type=MESH)
 
     def part_of(k):
-        return pl.ds(0, tok // 4) if k == 0 else pl.ds(tok // 4, tok - tok // 4)
+        at = (0, tok // 8, tok // 2, tok)
+        return pl.ds(at[k], at[k + 1] - at[k])
 
     def sub_load(k):
         owner = jnp.where(z < 2, 3, 0)
         at = part_of(k)
-        start = pl.multiple_of(owner * cols + at.start, tok // 4)
+        start = pl.multiple_of(owner * cols + at.start, tok // 8)
         return pltpu.make_async_copy(w_hbm.at[:, pl.ds(start, at.size)], w_buf.at[0, :, at], sub_w.at[k])
 
     @pl.when(inner)
@@ -203,6 +204,11 @@
     msg_copy = pltpu.make_async_remote_copy(src_ref=msg_src, dst_ref=msg_in, send_sem=msg_send, recv_sem=msg_recv,
                                             device_id={"hid": far}, device_id_type=MESH)
 
+    @pl.when(inner)
+    def _():
+        for k in range(SUB):
+            sub_copy(k).wait_recv()
+
     h_copy.wait()
     for k in range(SUB):
         sub_product(k)
@@ -249,6 +255,10 @@
             def _():
                 outer_copy(t).start()
 
+            @pl.when(t == 0)
+            def _():
+                sub_copy(1).wait_send()
+
             @pl.when(t < NP)
             def _():
                 products(i)
@@ -286,7 +296,7 @@
         lax.fori_loop(0, last, step, ())
         for k in range(NX):
             x_copy(k).start()
-        for k in range(SUB):
+        for k in (0, 2):
             sub_copy(k).wait_send()
         for k in range(RING):
             outer_copy(last - RING + k).wait_send()
@@ -297,11 +307,6 @@
         def step(t, _):
             i = lax.rem(t, NP)
             g = t - LAG
-
-            @pl.when(t == 0)
-            def _():
-                for k in range(SUB):
-                    sub_copy(k).wait_recv()
 
             @pl.when(t > 0)
             def _():
@@ -425,12 +430,12 @@
         res_copy.start()
         for i in range(NP - NX):
             spread(i, out_ref[:, i * tok:(i + 1) * tok], mult, shift)
+        for cross, dv in peers:
+            st_copy(slot, cross, dv).wait_send()
+        res_copy.wait_send()
         for k in range(NX):
             x_copy(k).wait_recv()
             spread(NP - NX + k, x_in[k], mult, shift)
-        for cross, dv in peers:
-            st_copy(slot, cross, dv).wait_send()
-        res_copy.wait_send()
 
     @pl.when(outer)
     def _():

time: 142 us -> 142 us (level)
  no operation moved by 1% of the time
where the time goes in v5:
time: 142 us
  Pallas kernels  141 us (99%)
    pallas_call x1, Pallas kernels, local_step(): pl.pallas_call(functools.partial(kernel, tok), out_shape=(pltpu.VMEM((row...  140 us

profile of v5, /device:TPU:16, one launch (start us, length us, event | category | flops | bytes accessed | tf_op | source)
XLA Modules:
  0.0 141.8 jit_solution(2772563638488186387)
XLA Ops:
  0.6 139.8 %head_cdf.1 = (f32[32,16384]{1,0:T(8,128)S(1)}, f32[1,32]{1,0:T(1,128)S(1)}) custom-call(bf16[32,288]{1,0:T(8,128)(2,1)} %h_hbm.1, bf16[288,65536]{1,0:T(8,128)(2,1)} %w_hbm.1, f32[1,32]{1,0:T(1,128)} %bitcast.3, s32[1,32]{1,0:T(1,128)} %bitcast.4), custom_call_target="tpu_custom_call" | custom-call | tf_op jit(solution)/shard_map/head_cdf/pallas_call | solution.py:473
  140.4 1.3 write.1

commit v6 on v5

--- a/solution.py
+++ b/solution.py
@@ -14,6 +14,7 @@
 LAG = 4
 XSTEP = 2 * NP - 3
 SUB = 3
+X_SENDS = ((0, 2), (2, 3), (5, 1))
 AHEAD = 2
 VMEM_LIMIT = 67043328 - 2 ** 21 - 2 ** 13
 F32 = jnp.float32
@@ -102,16 +103,19 @@
         product(2, i, 2)
         product(1, i, 3)
 
-        @pl.when(i + 1 < NP)
+        @pl.when(i + 2 < NP)
         def _():
-            product(3, i + 1, 0)
+            product(3, i + 2, 0)
 
     def sub_product(k):
         sub_load(k).wait()
         part[3 * NP, :, part_of(k)] = jnp.dot(h_buf[...], w_buf[0, :, part_of(k)], preferred_element_type=F32)
 
     def sub_copy(k):
-        return pltpu.make_async_remote_copy(src_ref=part.at[3 * NP, :, part_of(k)], dst_ref=far_in.at[0, :, part_of(k)],
+        src, dst = part.at[3 * NP + 1], far_in.at[1]
+        if k < SUB:
+            src, dst = part.at[3 * NP, :, part_of(k)], far_in.at[0, :, part_of(k)]
+        return pltpu.make_async_remote_copy(src_ref=src, dst_ref=dst,
                                             send_sem=sub_send.at[k], recv_sem=sub_recv.at[k],
                                             device_id={"hid": far}, device_id_type=MESH)
 
@@ -181,8 +185,10 @@
         i, ph = lax.rem(t, NP), t // NP
         return (3 - ph) * NP + jnp.where(ph == 1, lax.rem(i + NP - NX, NP), i)
 
-    def outer_copy(t):
-        return far_copy(part.at[part_index(t)], t, far_in, far_recv)
+    def outer_copy(u):
+        return pltpu.make_async_remote_copy(src_ref=part.at[pl.ds(part_index(2 * u), 2)], dst_ref=far_in.at[pl.ds(2 * u, 2)],
+                                            send_sem=far_send.at[lax.rem(u, RING)], recv_sem=far_recv.at[u],
+                                            device_id={"hid": far}, device_id_type=MESH)
 
     def inner_copy(t):
         return far_copy(far_in.at[t], t, side_in, side_recv)
@@ -197,9 +203,10 @@
                                             send_sem=xp_send.at[k], recv_sem=xp_recv.at[k],
                                             device_id={"hid": near}, device_id_type=MESH)
 
-    def x_copy(k):
-        return pltpu.make_async_remote_copy(src_ref=x_src.at[k], dst_ref=x_in.at[k], send_sem=x_send.at[k],
-                                            recv_sem=x_recv.at[k], device_id={"hid": far}, device_id_type=MESH)
+    def x_copy(j):
+        at = pl.ds(*X_SENDS[j])
+        return pltpu.make_async_remote_copy(src_ref=x_src.at[at], dst_ref=x_in.at[at], send_sem=x_send.at[j],
+                                            recv_sem=x_recv.at[j], device_id={"hid": far}, device_id_type=MESH)
 
     msg_copy = pltpu.make_async_remote_copy(src_ref=msg_src, dst_ref=msg_in, send_sem=msg_send, recv_sem=msg_recv,
                                             device_id={"hid": far}, device_id_type=MESH)
@@ -215,8 +222,9 @@
         if k == 0:
             for i in range(AHEAD):
                 for lane, rel in ((0, 3), (1, 0), (2, 2), (3, 1)):
-                    if i or lane:
-                        w_load(rel, i, lane).start()
+                    j = 1 - i if lane == 0 else i
+                    if j or lane:
+                        w_load(rel, j, lane).start()
 
             @pl.when(outer)
             def _():
@@ -227,6 +235,12 @@
             sub_copy(k).start()
 
     w_load(3, AHEAD, 0).start()
+    product(3, 1, 0)
+
+    @pl.when(outer)
+    def _():
+        sub_copy(SUB).start()
+
     temp_copy.wait()
     tgt_copy.wait()
     temp = to_col(temp_buf[...])
@@ -247,13 +261,15 @@
         def step(t, _):
             i = lax.rem(t, NP)
 
-            @pl.when(t > RING)
-            def _():
-                outer_copy(t - RING).wait_send()
-
-            @pl.when(t > 0)
-            def _():
-                outer_copy(t).start()
+            u = t // 2
+
+            @pl.when((t > 2 * RING) & (lax.rem(t, 2) == 0))
+            def _():
+                outer_copy(u - RING).wait_send()
+
+            @pl.when((t > 0) & (lax.rem(t, 2) == 0))
+            def _():
+                outer_copy(u).start()
 
             @pl.when(t == 0)
             def _():
@@ -294,12 +310,12 @@
             return ()
 
         lax.fori_loop(0, last, step, ())
-        for k in range(NX):
-            x_copy(k).start()
-        for k in (0, 2):
+        for j in range(len(X_SENDS)):
+            x_copy(j).start()
+        for k in (0, *range(2, SUB + 1)):
             sub_copy(k).wait_send()
         for k in range(RING):
-            outer_copy(last - RING + k).wait_send()
+            outer_copy(last // 2 - RING + k).wait_send()
         msg_copy.wait_send()
 
     @pl.when(inner)
@@ -308,9 +324,13 @@
             i = lax.rem(t, NP)
             g = t - LAG
 
-            @pl.when(t > 0)
-            def _():
-                far_copy(far_in.at[t], t, far_in, far_recv).wait_recv()
+            @pl.when(t == 1)
+            def _():
+                sub_copy(SUB).wait_recv()
+
+            @pl.when((t > 1) & (lax.rem(t, 2) == 0))
+            def _():
+                outer_copy(t // 2).wait_recv()
 
             @pl.when((t >= 1) & (t <= 2 * NP))
             def _():
@@ -433,9 +453,10 @@
         for cross, dv in peers:
             st_copy(slot, cross, dv).wait_send()
         res_copy.wait_send()
-        for k in range(NX):
-            x_copy(k).wait_recv()
-            spread(NP - NX + k, x_in[k], mult, shift)
+        for j, (first, count) in enumerate(X_SENDS):
+            x_copy(j).wait_recv()
+            for k in range(first, first + count):
+                spread(NP - NX + k, x_in[k], mult, shift)
 
     @pl.when(outer)
     def _():
@@ -445,8 +466,8 @@
         mult, shift = settle(res[0:1], res[1:2], res[2:3])
         for i in range(NP):
             spread(i, out_ref[:, i * tok:(i + 1) * tok], mult, shift)
-        for k in range(NX):
-            x_copy(k).wait_send()
+        for j in range(len(X_SENDS)):
+            x_copy(j).wait_send()
 
 
 def write_kernel(table_ref, at_tgt_ref, table_hbm, at_tgt_hbm, sem, at_sem):
@@ -490,10 +511,10 @@
                 vmem((32, 128), F32),
                 vmem((8, 128), F32), vmem((8, 128), F32), vmem((8, 8, 128), F32),
                 vmem((8, 128), F32), vmem((8, 128), F32),
-                dma, dma, dma, dma((4 * AHEAD,)), dma((SUB,)), dma((SUB,)), dma((SUB,)),
-                dma((RING,)), dma((3 * NP,)), dma((2 * NP,)),
+                dma, dma, dma, dma((4 * AHEAD,)), dma((SUB,)), dma((SUB + 1,)), dma((SUB + 1,)),
+                dma((RING,)), dma((3 * NP // 2,)), dma((2 * NP,)),
                 dma((RING,)), dma((NP,)),
-                dma((NX,)), dma((NX,)), dma((NX,)), dma((NX,)),
+                dma((NX,)), dma((NX,)), dma((len(X_SENDS),)), dma((len(X_SENDS),)),
                 dma, dma, dma((8,)), dma((8,)), dma, dma, pltpu.SemaphoreType.REGULAR,
             ],
             compiler_params=pltpu.CompilerParams(collective_id=0, has_side_effects=True, vmem_limit_bytes=VMEM_LIMIT),

time: 142 us -> 142 us (level)
  no operation moved by 1% of the time
where the time goes in v6:
time: 142 us
  Pallas kernels  141 us (99%)
    pallas_call x1, Pallas kernels, local_step(): pl.pallas_call(functools.partial(kernel, tok), out_shape=(pltpu.VMEM((row...  140 us

profile of v6, /device:TPU:16, one launch (start us, length us, event | category | flops | bytes accessed | tf_op | source)
XLA Modules:
  0.0 141.5 jit_solution(12740642923786548614)
XLA Ops:
  0.6 139.5 %head_cdf.1 = (f32[32,16384]{1,0:T(8,128)S(1)}, f32[1,32]{1,0:T(1,128)S(1)}) custom-call(bf16[32,288]{1,0:T(8,128)(2,1)} %h_hbm.1, bf16[288,65536]{1,0:T(8,128)(2,1)} %w_hbm.1, f32[1,32]{1,0:T(1,128)} %bitcast.3, s32[1,32]{1,0:T(1,128)} %bitcast.4), custom_call_target="tpu_custom_call" | custom-call | tf_op jit(solution)/shard_map/head_cdf/pallas_call | solution.py:494
  140.2 1.3 write.1

commit v7 on v6

--- a/solution.py
+++ b/solution.py
@@ -14,6 +14,7 @@
 LAG = 4
 XSTEP = 2 * NP - 3
 SUB = 3
+SENDS = (*((t, 2) for t in range(2, NP, 2)), (16, 6), (22, 5), (27, 5), (32, 5), (37, 5))
 X_SENDS = ((0, 2), (2, 3), (5, 1))
 AHEAD = 2
 VMEM_LIMIT = 67043328 - 2 ** 21 - 2 ** 13
@@ -39,7 +40,7 @@
 def kernel(tok, h_hbm, w_hbm, temp_hbm, tgt_hbm, out_ref, tgt_out_ref,
            h_buf, temp_buf, tgt_buf, w_buf, part, far_in, side_in, near_in, x_part, x_src, x_in, piece_m, piece_s, piece_t,
            msg_src, msg_in, stats, res_src, res_in,
-           h_sem, temp_sem, tgt_sem, w_sem, sub_w, sub_send, sub_recv, far_send, far_recv, side_recv, near_send, near_recv, xp_send, xp_recv, x_send, x_recv,
+           h_sem, temp_sem, tgt_sem, w_sem, sub_w, sub_send, sub_recv, out_send, far_send, far_recv, side_recv, near_send, near_recv, xp_send, xp_recv, x_send, x_recv,
            msg_send, msg_recv, st_send, st_recv, res_send, res_recv, ready):
     z, v = lax.axis_index("hid"), lax.axis_index("vocab")
     outer = (z == 0) | (z == 3)
@@ -185,9 +186,10 @@
         i, ph = lax.rem(t, NP), t // NP
         return (3 - ph) * NP + jnp.where(ph == 1, lax.rem(i + NP - NX, NP), i)
 
-    def outer_copy(u):
-        return pltpu.make_async_remote_copy(src_ref=part.at[pl.ds(part_index(2 * u), 2)], dst_ref=far_in.at[pl.ds(2 * u, 2)],
-                                            send_sem=far_send.at[lax.rem(u, RING)], recv_sem=far_recv.at[u],
+    def outer_copy(j):
+        t, count = SENDS[j]
+        return pltpu.make_async_remote_copy(src_ref=part.at[pl.ds(part_index(t), count)], dst_ref=far_in.at[pl.ds(t, count)],
+                                            send_sem=out_send.at[j], recv_sem=far_recv.at[j],
                                             device_id={"hid": far}, device_id_type=MESH)
 
     def inner_copy(t):
@@ -261,15 +263,12 @@
         def step(t, _):
             i = lax.rem(t, NP)
 
-            u = t // 2
-
-            @pl.when((t > 2 * RING) & (lax.rem(t, 2) == 0))
-            def _():
-                outer_copy(u - RING).wait_send()
-
-            @pl.when((t > 0) & (lax.rem(t, 2) == 0))
-            def _():
-                outer_copy(u).start()
+            for j, (first, _) in enumerate(SENDS):
+                @pl.when(t == first)
+                def _(j=j):
+                    if j >= RING:
+                        outer_copy(j - RING).wait_send()
+                    outer_copy(j).start()
 
             @pl.when(t == 0)
             def _():
@@ -315,7 +314,7 @@
         for k in (0, *range(2, SUB + 1)):
             sub_copy(k).wait_send()
         for k in range(RING):
-            outer_copy(last // 2 - RING + k).wait_send()
+            outer_copy(len(SENDS) - RING + k).wait_send()
         msg_copy.wait_send()
 
     @pl.when(inner)
@@ -328,9 +327,10 @@
             def _():
                 sub_copy(SUB).wait_recv()
 
-            @pl.when((t > 1) & (lax.rem(t, 2) == 0))
-            def _():
-                outer_copy(t // 2).wait_recv()
+            for j, (first, _) in enumerate(SENDS):
+                @pl.when(t == first)
+                def _(j=j):
+                    outer_copy(j).wait_recv()
 
             @pl.when((t >= 1) & (t <= 2 * NP))
             def _():
@@ -511,8 +511,8 @@
                 vmem((32, 128), F32),
                 vmem((8, 128), F32), vmem((8, 128), F32), vmem((8, 8, 128), F32),
                 vmem((8, 128), F32), vmem((8, 128), F32),
-                dma, dma, dma, dma((4 * AHEAD,)), dma((SUB,)), dma((SUB + 1,)), dma((SUB + 1,)),
-                dma((RING,)), dma((3 * NP // 2,)), dma((2 * NP,)),
+                dma, dma, dma, dma((4 * AHEAD,)), dma((SUB,)), dma((SUB + 1,)), dma((SUB + 1,)), dma((len(SENDS),)),
+                dma((RING,)), dma((len(SENDS),)), dma((2 * NP,)),
                 dma((RING,)), dma((NP,)),
                 dma((NX,)), dma((NX,)), dma((len(X_SENDS),)), dma((len(X_SENDS),)),
                 dma, dma, dma((8,)), dma((8,)), dma, dma, pltpu.SemaphoreType.REGULAR,

time: 142 us -> 142 us (level)
  no operation moved by 1% of the time
where the time goes in v7:
time: 142 us
  Pallas kernels  141 us (99%)
    pallas_call x1, Pallas kernels, local_step(): pl.pallas_call(functools.partial(kernel, tok), out_shape=(pltpu.VMEM((row...  140 us

profile of v7, /device:TPU:16, one launch (start us, length us, event | category | flops | bytes accessed | tf_op | source)
XLA Modules:
  0.0 141.5 jit_solution(10895403576541209477)
XLA Ops:
  0.6 139.5 %head_cdf.1 = (f32[32,16384]{1,0:T(8,128)S(1)}, f32[1,32]{1,0:T(1,128)S(1)}) custom-call(bf16[32,288]{1,0:T(8,128)(2,1)} %h_hbm.1, bf16[288,65536]{1,0:T(8,128)(2,1)} %w_hbm.1, f32[1,32]{1,0:T(1,128)} %bitcast.3, s32[1,32]{1,0:T(1,128)} %bitcast.4), custom_call_target="tpu_custom_call" | custom-call | tf_op jit(solution)/shard_map/head_cdf/pallas_call | solution.py:494
  140.2 1.3 write.1

commit v8 on v7

--- a/solution.py
+++ b/solution.py
@@ -15,7 +15,7 @@
 XSTEP = 2 * NP - 3
 SUB = 3
 SENDS = (*((t, 2) for t in range(2, NP, 2)), (16, 6), (22, 5), (27, 5), (32, 5), (37, 5))
-X_SENDS = ((0, 2), (2, 3), (5, 1))
+X_SENDS = ((0, 5), (5, 1))
 AHEAD = 2
 VMEM_LIMIT = 67043328 - 2 ** 21 - 2 ** 13
 F32 = jnp.float32

time: 142 us -> 142 us (level)
  no operation moved by 1% of the time
where the time goes in v8:
time: 142 us
  Pallas kernels  141 us (99%)
    pallas_call x1, Pallas kernels, local_step(): pl.pallas_call(functools.partial(kernel, tok), out_shape=(pltpu.VMEM((row...  140 us

profile of v8, /device:TPU:16, one launch (start us, length us, event | category | flops | bytes accessed | tf_op | source)
XLA Modules:
  0.0 141.5 jit_solution(12332746792305626925)
XLA Ops:
  0.6 139.5 %head_cdf.1 = (f32[32,16384]{1,0:T(8,128)S(1)}, f32[1,32]{1,0:T(1,128)S(1)}) custom-call(bf16[32,288]{1,0:T(8,128)(2,1)} %h_hbm.1, bf16[288,65536]{1,0:T(8,128)(2,1)} %w_hbm.1, f32[1,32]{1,0:T(1,128)} %bitcast.3, s32[1,32]{1,0:T(1,128)} %bitcast.4), custom_call_target="tpu_custom_call" | custom-call | tf_op jit(solution)/shard_map/head_cdf/pallas_call | solution.py:494
  140.2 1.3 write.1

commit v9 on v8

--- a/solution.py
+++ b/solution.py
@@ -65,7 +65,7 @@
         pl.semaphore_signal(barrier, inc=1, device_id=dev, device_id_type=MESH)
 
     def part_of(k):
-        at = (0, tok // 8, tok // 2, tok)
+        at = (0, tok // 8, 3 * tok // 8, tok)
         return pl.ds(at[k], at[k + 1] - at[k])
 
     def sub_load(k):

time: 142 us -> 142 us (level)
  no operation moved by 1% of the time
where the time goes in v9:
time: 142 us
  Pallas kernels  141 us (99%)
    pallas_call x1, Pallas kernels, local_step(): pl.pallas_call(functools.partial(kernel, tok), out_shape=(pltpu.VMEM((row...  140 us

profile of v9, /device:TPU:16, one launch (start us, length us, event | category | flops | bytes accessed | tf_op | source)
XLA Modules:
  0.0 141.5 jit_solution(17150252022591724647)
XLA Ops:
  0.6 139.5 %head_cdf.1 = (f32[32,16384]{1,0:T(8,128)S(1)}, f32[1,32]{1,0:T(1,128)S(1)}) custom-call(bf16[32,288]{1,0:T(8,128)(2,1)} %h_hbm.1, bf16[288,65536]{1,0:T(8,128)(2,1)} %w_hbm.1, f32[1,32]{1,0:T(1,128)} %bitcast.3, s32[1,32]{1,0:T(1,128)} %bitcast.4), custom_call_target="tpu_custom_call" | custom-call | tf_op jit(solution)/shard_map/head_cdf/pallas_call | solution.py:494
  140.2 1.3 write.1
